TPU v7x, 32 devices: a whole 2x2x4 slice. The times are simulated.
32 devices in a mesh: row: 8 (over y, x, core), col: 4 (over z).
Axes of the slice: x: 2, y: 2, z: 4, core: 2. Of those that a mesh axis runs over, the one named last changes fastest.
Arguments:
- row_cells: int32 [3, 8192], P(None, 'row'), may hold values from 0 to 63
- col_cells: int32 [3, 32768], P(None, 'col'), may hold values from 0 to 63
- omega: float32 [16, 32768], P(None, 'col'), may hold values from -6 to 6
Outputs:
- basis: float32 [16, 8192], P(None, 'row')
- image: float32 [16, 32768], P(None, 'col')
- core: float32 [16, 16], replicated
All inputs are finite; a program needn't handle non-finite values.
Results may differ from a plain program's by a relative error of at most 0.0001.
Values sent between devices are 32-bit elements; how exact they have to be, the bound alone decides.
A program may use at most 64 MiB of HBM per device.

v0:
```python
import jax
import jax.numpy as jnp
from jax import lax
from jax.sharding import PartitionSpec as P


def kernel_tile(rows, cols):
    first = (rows[0][:, None] - cols[0][None, :]).astype(jnp.float32)
    total = first * first
    second = (rows[1][:, None] - cols[1][None, :]).astype(jnp.float32)
    total = total + second * second
    third = (rows[2][:, None] - cols[2][None, :]).astype(jnp.float32)
    total = total + third * third
    return 0.25 * jnp.exp(-jnp.sqrt(total) / 6.4)


def shards(row_cells, col_cells, omega):
    rank = omega.shape[0]
    local_rows = row_cells.shape[1]
    local_cols = col_cells.shape[1]
    rows_total = local_rows * lax.axis_size("row")
    order = local_cols * lax.axis_size("col")
    width = min(local_cols, 2048)
    count = local_cols // width

    def tile_at(index):
        cols = lax.dynamic_slice_in_dim(col_cells, index * width, width, 1)
        return kernel_tile(row_cells, cols)

    tiles = lax.map(tile_at, jnp.arange(count, dtype=jnp.int32))
    sketch_part = jnp.einsum(
        "kbw,bmw->km", omega.reshape(rank, count, width), tiles, precision=lax.Precision.HIGHEST
    )
    sketch = lax.psum(sketch_part, "col")
    gram = lax.psum(jnp.dot(sketch, sketch.T, precision=lax.Precision.HIGHEST), "row") / rows_total
    lower = jnp.linalg.cholesky(gram)
    basis = jax.scipy.linalg.solve_triangular(lower, sketch, lower=True)
    image_part = jnp.einsum("km,bmw->kbw", basis, tiles, precision=lax.Precision.HIGHEST).reshape(
        rank, local_cols
    )
    image = lax.psum(image_part, "row")
    core = lax.psum(jnp.dot(image, image.T, precision=lax.Precision.HIGHEST), "col") / order
    return (basis, image, core)


def solution(mesh):
    return jax.shard_map(
        shards,
        mesh=mesh,
        in_specs=(P(None, "row"), P(None, "col"), P(None, "col")),
        out_specs=(P(None, "row"), P(None, "col"), P()),
        check_vma=False,
    )
```

profile of v0, /device:TPU:0, one launch (start us, length us, event | category | flops | bytes accessed | tf_op | source)
XLA Modules:
  0.0 236.3 jit_solution(15518683551914293562)
XLA Ops:
  7.2 0.0 all-reduce.3.cloned.1.call-start
  7.2 0.0 copy-start
  7.2 43.4 %while.10 = (s32[]{:T(128)}, f32[4,1024,2048]{2,1,0:T(8,128)}, s32[3,1024]{1,0:T(4,128)}, s32[4]{0:T(128)S(1)}, s32[3,8192]{1,0:T(4,128)}, /*index=5*/s32[]{:T(1...) while((s32[]{:T(128)}, f32[4,1024,2048]{2,1,0:T(8,128)}, s32[3,1024]{1,0:T(4,128)}, ...), condition=%wide.region_1.2_spmd, body=%wide.region_0.1_spmd.sunk | while | flops 29360136 | bytes 8499915 | solution.py:30
  7.3 0.6 dynamic_slice.8
  8.5 1.0 constant_dynamic-slice_fusion.2
  9.5 0.8 fusion.18
  10.3 7.8 %multiply_dynamic-update-slice_fusion.2 = f32[4,1024,2048]{2,1,0:T(8,128)} fusion(f32[4,1024,2048]{2,1,0:T(8,128)} %get-tuple-element.102, s32[]{:T(128)} %get-tuple-element.101, s32[2048]{0:T(1024)S(1)} %bitcast.54, s32[1024]{0:T(1024)S(1)} %bitcast.57, s32[2048]{0:T(1024)S(1)} %bitcast.53, s32[1024]{0:T(1024)S(1)} %bitcast.58, s32[2048]{0:T(1024)S(1)} %bitcast.52, ...), kind=kLoop, calls=%fused_computation.clone.1 | loop fusion | flops 29360128 | bytes 8425984 | tf_op jit(solution)/shard_map/while/body/jit(dynamic_update_index_in_dim)/dynamic_update_slice | solution.py:30
  18.1 0.6 dynamic_slice.8
  19.4 1.0 constant_dynamic-slice_fusion.2
  20.3 0.8 fusion.18
  21.2 7.8 %multiply_dynamic-update-slice_fusion.2 = f32[4,1024,2048]{2,1,0:T(8,128)} fusion(f32[4,1024,2048]{2,1,0:T(8,128)} %get-tuple-element.102, s32[]{:T(128)} %get-tuple-element.101, s32[2048]{0:T(1024)S(1)} %bitcast.54, s32[1024]{0:T(1024)S(1)} %bitcast.57, s32[2048]{0:T(1024)S(1)} %bitcast.53, s32[1024]{0:T(1024)S(1)} %bitcast.58, s32[2048]{0:T(1024)S(1)} %bitcast.52, ...), kind=kLoop, calls=%fused_computation.clone.1 | loop fusion | flops 29360128 | bytes 8425984 | tf_op jit(solution)/shard_map/while/body/jit(dynamic_update_index_in_dim)/dynamic_update_slice | solution.py:30
  29.0 0.6 dynamic_slice.8
  30.2 1.0 constant_dynamic-slice_fusion.2
  31.2 0.8 fusion.18
  32.0 7.8 %multiply_dynamic-update-slice_fusion.2 = f32[4,1024,2048]{2,1,0:T(8,128)} fusion(f32[4,1024,2048]{2,1,0:T(8,128)} %get-tuple-element.102, s32[]{:T(128)} %get-tuple-element.101, s32[2048]{0:T(1024)S(1)} %bitcast.54, s32[1024]{0:T(1024)S(1)} %bitcast.57, s32[2048]{0:T(1024)S(1)} %bitcast.53, s32[1024]{0:T(1024)S(1)} %bitcast.58, s32[2048]{0:T(1024)S(1)} %bitcast.52, ...), kind=kLoop, calls=%fused_computation.clone.1 | loop fusion | flops 29360128 | bytes 8425984 | tf_op jit(solution)/shard_map/while/body/jit(dynamic_update_index_in_dim)/dynamic_update_slice | solution.py:30
  39.8 0.6 dynamic_slice.8
  41.1 1.0 constant_dynamic-slice_fusion.2
  42.0 0.8 fusion.18
  42.9 7.8 %multiply_dynamic-update-slice_fusion.2 = f32[4,1024,2048]{2,1,0:T(8,128)} fusion(f32[4,1024,2048]{2,1,0:T(8,128)} %get-tuple-element.102, s32[]{:T(128)} %get-tuple-element.101, s32[2048]{0:T(1024)S(1)} %bitcast.54, s32[1024]{0:T(1024)S(1)} %bitcast.57, s32[2048]{0:T(1024)S(1)} %bitcast.53, s32[1024]{0:T(1024)S(1)} %bitcast.58, s32[2048]{0:T(1024)S(1)} %bitcast.52, ...), kind=kLoop, calls=%fused_computation.clone.1 | loop fusion | flops 29360128 | bytes 8425984 | tf_op jit(solution)/shard_map/while/body/jit(dynamic_update_index_in_dim)/dynamic_update_slice | solution.py:30
  50.6 0.0 copy-done
  50.7 32.5 %convolution_bitcast_fusion.1 = f32[16,1024]{1,0:T(8,128)} fusion(f32[4,1024,2048]{2,1,0:T(8,128)} %get-tuple-element.30, f32[2,4,8,2048]{3,2,1,0:T(8,128)S(1)} %bitcast.55), kind=kOutput, calls=%fused_computation.3 | convolution fusion | flops 1610612736 | bytes 34144256 | tf_op jit(solution)/shard_map/kbw,bmw->km/dot_general | solution.py:31
  83.2 0.0 all-reduce.3.cloned.1.call-update
  83.2 0.0 all-reduce.5.cloned.1.call-start
  83.2 37.1 %all-reduce.3.cloned.1.call-done = f32[16,1024]{1,0:T(8,128)} async-done(((f32[16,1024]{1,0:T(8,128)}), f32[16,1024]{1,0:T(8,128)}) %all-reduce.3.cloned.1.call-update) | async-done | bytes 65552 | tf_op jit(solution)/shard_map/psum | solution.py:34
  120.4 1.1 fusion.8
  121.4 12.3 %psum.29 = f32[16,16]{0,1:T(8,128)S(1)} all-reduce(f32[16,16]{0,1:T(8,128)S(1)} %fusion.8), channel_id=1, replica_groups=mesh['row'=8,'col'=4] {'row'}, use_global_device_ids=true, to_apply=%region_3.4 | all-reduce | flops 256 | bytes 2048 | tf_op jit(solution)/shard_map/psum | solution.py:35
  133.8 0.1 copy.11
  133.9 1.5 cholesky.16
  135.4 0.6 compare_reduce_fusion
  136.0 0.6 fusion.3
  136.7 1.2 custom-call.7
  137.9 1.1 fusion.4
  139.0 0.0 copy-start.1
  139.0 19.6 %convolution_bitcast_fusion = f32[4,2,8,2048]{3,2,1,0:T(8,128)S(1)} fusion(f32[4,1024,2048]{2,1,0:T(8,128)} %get-tuple-element.30, f32[16,1024]{1,0:T(8,128)S(1)} %fusion.4), kind=kOutput, calls=%fused_computation.2 | convolution fusion | flops 1610612736 | bytes 34144256 | tf_op jit(solution)/shard_map/km,bmw->kbw/dot_general | solution.py:38
  158.6 0.0 copy-done.1
  158.6 0.8 copy.15
  159.4 0.0 all-reduce.5.cloned.1.call-update
  159.5 53.8 %all-reduce.5.cloned.1.call-done = f32[16,8192]{1,0:T(8,128)} async-done(((f32[16,8192]{1,0:T(8,128)}), f32[16,8192]{1,0:T(8,128)}) %all-reduce.5.cloned.1.call-update) | async-done | bytes 524304 | tf_op jit(solution)/shard_map/psum | solution.py:41
  213.2 1.9 fusion.9
  215.2 11.8 %psum.31 = f32[16,16]{1,0:T(8,128)S(1)} all-reduce(f32[16,16]{1,0:T(8,128)S(1)} %fusion.9), channel_id=1, replica_groups=mesh['row'=8,'col'=4] {'col'}, use_global_device_ids=true, to_apply=%region_7.8 | all-reduce | flops 256 | bytes 2048 | tf_op jit(solution)/shard_map/psum | solution.py:42
  227.0 0.6 broadcast_multiply_fusion
  227.6 1.9 copy.29
  (5 shorter events, 0.0 us)
Async XLA Ops:
  7.2 113.2 %all-reduce.3.cloned.1.call-start = ((), (), s32[]{:S(2)}) async-start(), calls=%async_computation | async-start | bytes 131072 | tf_op jit(solution)/shard_map/psum | solution.py:34
  7.2 43.4 %copy-start = (f32[16,8192]{1,0:T(8,128)S(1)}, f32[16,8192]{1,0:T(8,128)}, u32[]{:S(2)}) copy-start(f32[16,8192]{1,0:T(8,128)} %param.7) | copy-start | bytes 1572868
  83.2 130.0 %all-reduce.5.cloned.1.call-start = ((), (), s32[]{:S(2)}) async-start(), calls=%async_computation.1 | async-start | bytes 1048576 | tf_op jit(solution)/shard_map/psum | solution.py:41
  139.0 19.6 %copy-start.1 = (f32[16,1024]{1,0:T(8,128)}, f32[16,1024]{1,0:T(8,128)S(1)}, u32[]{:S(2)}) copy-start(f32[16,1024]{1,0:T(8,128)S(1)} %fusion.4) | copy-start | bytes 196612
Sparse Core Ops, SparseCore 0:
  83.3 37.0 all-reduce.2
  159.6 53.5 all-reduce.4
where the time goes:
time: 237 us; the launch traced here: 236 us
  waiting for transfers between devices  90.9 us (38%)
  matrix products  56.2 us (24%)
  other arithmetic  35.7 us (15%)
  blocking collectives  24.1 us (10%)
  between operations  14.1 us (6%)
  local copies, waits for them, and re-layouts  12.4 us (5%)
  loops' own time  2.68 us (1%)
    psum x1, waiting for transfers between devices, shards(): image = lax.psum(image_part, 'row')  53.8 us
    psum x1, waiting for transfers between devices, shards(): sketch = lax.psum(sketch_part, 'col')  37.1 us
    dot_general x1, matrix products, shards(): jnp.einsum('kbw,bmw->km', omega.reshape(rank, count, width), tiles, preci...  32.5 us
    dynamic_update_slice x4, other arithmetic, shards(): tiles = lax.map(tile_at, jnp.arange(count, dtype=jnp.int32))  31.1 us
    dot_general x1, matrix products, shards(): jnp.einsum('km,bmw->kbw', basis, tiles, precision=lax.Precision.HIGHEST)  19.6 us
    psum x1, blocking collectives, shards(): lax.psum(jnp.dot(sketch, sketch.T, precision=lax.Precision.HIGHEST), 'row')  12.3 us
    psum x1, blocking collectives, shards(): lax.psum(jnp.dot(image, image.T, precision=lax.Precision.HIGHEST), 'col')  11.8 us
    slice x8, local copies, waits for them, and re-layouts, kernel_tile(): first = (rows[0][:, None] - cols[0][None, :]).astype(jnp.float32)  7.27 us
  transfers between devices with their start and end apart: 2, of which 2 were waited for; matrix products, arithmetic and copies ran while one was open for 0% of the time, Pallas kernels for 0%

commit v1 on v0

--- a/solution.py
+++ b/solution.py
@@ -31,7 +31,8 @@
     sketch_part = jnp.einsum(
         "kbw,bmw->km", omega.reshape(rank, count, width), tiles, precision=lax.Precision.HIGHEST
     )
-    sketch = lax.psum(sketch_part, "col")
+    terms = lax.all_gather(sketch_part, "col")
+    sketch = jnp.sum(terms, axis=0)
     gram = lax.psum(jnp.dot(sketch, sketch.T, precision=lax.Precision.HIGHEST), "row") / rows_total
     lower = jnp.linalg.cholesky(gram)
     basis = jax.scipy.linalg.solve_triangular(lower, sketch, lower=True)

time: 237 us -> 213 us (0.90)
  waiting for transfers between devices: 90.9 us -> 55.5 us
  blocking collectives: 24.1 us -> 39.9 us
  matrix products: 56.2 us -> 51.8 us
    psum x1 -> x0, waiting for transfers between devices: 37.1 us -> none  [shards(): sketch = lax.psum(sketch_part, 'col')]
    all_gather x0 -> x1, blocking collectives: none -> 15.7 us  [shards(): terms = lax.all_gather(sketch_part, 'col')]
    dot_general x1, matrix products: 32.5 us -> 29.8 us  [shards(): jnp.einsum('kbw,bmw->km', omega.reshape(rank, count, width), tiles, preci...]
  transfers between devices with their start and end apart: 2 -> 1, of which waited for: 2 -> 1; matrix products, arithmetic and copies ran while one was open for 0% -> 0% of each run, Pallas kernels for 0% -> 0%
where the time goes in v1:
time: 213 us; the launch traced here: 212 us
  waiting for transfers between devices  55.5 us (26%)
  matrix products  51.8 us (24%)
  blocking collectives  39.9 us (19%)
  other arithmetic  35.8 us (17%)
  between operations  14.1 us (7%)
  local copies, waits for them, and re-layouts  12.4 us (6%)
  loops' own time  2.68 us (1%)
    psum x1, waiting for transfers between devices, shards(): image = lax.psum(image_part, 'row')  55.5 us
    dynamic_update_slice x4, other arithmetic, shards(): tiles = lax.map(tile_at, jnp.arange(count, dtype=jnp.int32))  31.1 us
    dot_general x1, matrix products, shards(): jnp.einsum('kbw,bmw->km', omega.reshape(rank, count, width), tiles, preci...  29.8 us
    dot_general x1, matrix products, shards(): jnp.einsum('km,bmw->kbw', basis, tiles, precision=lax.Precision.HIGHEST)  19.6 us
    all_gather x1, blocking collectives, shards(): terms = lax.all_gather(sketch_part, 'col')  15.7 us
    psum x1, blocking collectives, shards(): lax.psum(jnp.dot(sketch, sketch.T, precision=lax.Precision.HIGHEST), 'row')  12.4 us
    psum x1, blocking collectives, shards(): lax.psum(jnp.dot(image, image.T, precision=lax.Precision.HIGHEST), 'col')  11.8 us
    slice x8, local copies, waits for them, and re-layouts, kernel_tile(): first = (rows[0][:, None] - cols[0][None, :]).astype(jnp.float32)  7.27 us
  transfers between devices with their start and end apart: 1, of which 1 were waited for; matrix products, arithmetic and copies ran while one was open for 0% of the time, Pallas kernels for 0%

profile of v1, /device:TPU:0, one launch (start us, length us, event | category | flops | bytes accessed | tf_op | source)
XLA Modules:
  0.0 212.2 jit_solution(17949065155297085237)
XLA Ops:
  7.2 0.0 all-reduce.2.cloned.1.call-start
  7.2 0.0 copy-start
  7.2 43.4 %while.10 = (s32[]{:T(128)}, f32[4,1024,2048]{2,1,0:T(8,128)}, s32[3,1024]{1,0:T(4,128)}, s32[4]{0:T(128)S(1)}, s32[3,8192]{1,0:T(4,128)}, /*index=5*/s32[]{:T(1...) while((s32[]{:T(128)}, f32[4,1024,2048]{2,1,0:T(8,128)}, s32[3,1024]{1,0:T(4,128)}, ...), condition=%wide.region_1.2_spmd, body=%wide.region_0.1_spmd.sunk | while | flops 29360136 | bytes 8499915 | solution.py:30
  7.3 0.6 dynamic_slice.8
  8.5 1.0 constant_dynamic-slice_fusion.2
  9.5 0.8 fusion.18
  10.3 7.8 %multiply_dynamic-update-slice_fusion.2 = f32[4,1024,2048]{2,1,0:T(8,128)} fusion(f32[4,1024,2048]{2,1,0:T(8,128)} %get-tuple-element.102, s32[]{:T(128)} %get-tuple-element.101, s32[2048]{0:T(1024)S(1)} %bitcast.56, s32[1024]{0:T(1024)S(1)} %bitcast.59, s32[2048]{0:T(1024)S(1)} %bitcast.55, s32[1024]{0:T(1024)S(1)} %bitcast.60, s32[2048]{0:T(1024)S(1)} %bitcast.54, ...), kind=kLoop, calls=%fused_computation.clone.1 | loop fusion | flops 29360128 | bytes 8425984 | tf_op jit(solution)/shard_map/while/body/jit(dynamic_update_index_in_dim)/dynamic_update_slice | solution.py:30
  18.1 0.6 dynamic_slice.8
  19.4 1.0 constant_dynamic-slice_fusion.2
  20.3 0.8 fusion.18
  21.2 7.8 %multiply_dynamic-update-slice_fusion.2 = f32[4,1024,2048]{2,1,0:T(8,128)} fusion(f32[4,1024,2048]{2,1,0:T(8,128)} %get-tuple-element.102, s32[]{:T(128)} %get-tuple-element.101, s32[2048]{0:T(1024)S(1)} %bitcast.56, s32[1024]{0:T(1024)S(1)} %bitcast.59, s32[2048]{0:T(1024)S(1)} %bitcast.55, s32[1024]{0:T(1024)S(1)} %bitcast.60, s32[2048]{0:T(1024)S(1)} %bitcast.54, ...), kind=kLoop, calls=%fused_computation.clone.1 | loop fusion | flops 29360128 | bytes 8425984 | tf_op jit(solution)/shard_map/while/body/jit(dynamic_update_index_in_dim)/dynamic_update_slice | solution.py:30
  29.0 0.6 dynamic_slice.8
  30.2 1.0 constant_dynamic-slice_fusion.2
  31.2 0.8 fusion.18
  32.0 7.8 %multiply_dynamic-update-slice_fusion.2 = f32[4,1024,2048]{2,1,0:T(8,128)} fusion(f32[4,1024,2048]{2,1,0:T(8,128)} %get-tuple-element.102, s32[]{:T(128)} %get-tuple-element.101, s32[2048]{0:T(1024)S(1)} %bitcast.56, s32[1024]{0:T(1024)S(1)} %bitcast.59, s32[2048]{0:T(1024)S(1)} %bitcast.55, s32[1024]{0:T(1024)S(1)} %bitcast.60, s32[2048]{0:T(1024)S(1)} %bitcast.54, ...), kind=kLoop, calls=%fused_computation.clone.1 | loop fusion | flops 29360128 | bytes 8425984 | tf_op jit(solution)/shard_map/while/body/jit(dynamic_update_index_in_dim)/dynamic_update_slice | solution.py:30
  39.8 0.6 dynamic_slice.8
  41.1 1.0 constant_dynamic-slice_fusion.2
  42.0 0.8 fusion.18
  42.9 7.8 %multiply_dynamic-update-slice_fusion.2 = f32[4,1024,2048]{2,1,0:T(8,128)} fusion(f32[4,1024,2048]{2,1,0:T(8,128)} %get-tuple-element.102, s32[]{:T(128)} %get-tuple-element.101, s32[2048]{0:T(1024)S(1)} %bitcast.56, s32[1024]{0:T(1024)S(1)} %bitcast.59, s32[2048]{0:T(1024)S(1)} %bitcast.55, s32[1024]{0:T(1024)S(1)} %bitcast.60, s32[2048]{0:T(1024)S(1)} %bitcast.54, ...), kind=kLoop, calls=%fused_computation.clone.1 | loop fusion | flops 29360128 | bytes 8425984 | tf_op jit(solution)/shard_map/while/body/jit(dynamic_update_index_in_dim)/dynamic_update_slice | solution.py:30
  50.6 0.0 copy-done
  50.7 29.8 %convolution_bitcast_fusion.1 = f32[16,1024]{1,0:T(8,128)S(1)} fusion(f32[4,1024,2048]{2,1,0:T(8,128)} %get-tuple-element.30, f32[2,4,8,2048]{3,2,1,0:T(8,128)S(1)} %bitcast.57), kind=kOutput, calls=%fused_computation.3 | convolution fusion | flops 1610612736 | bytes 34144256 | tf_op jit(solution)/shard_map/kbw,bmw->km/dot_general | solution.py:31
  80.5 15.7 %all-gather = f32[64,1024]{1,0:T(8,128)S(1)} all-gather(f32[16,1024]{1,0:T(8,128)S(1)} %convolution_bitcast_fusion.1), channel_id=2, replica_groups=mesh['row'=8,'col'=4] {'col'}, dimensions={0}, use_global_device_ids=true | all-gather | bytes 327680 | tf_op jit(solution)/shard_map/all_gather | solution.py:34
  96.2 0.2 fusion.8
  96.3 12.4 %psum.21 = f32[16,16]{0,1:T(8,128)S(1)} all-reduce(f32[16,16]{0,1:T(8,128)S(1)} %fusion.8), channel_id=1, replica_groups=mesh['row'=8,'col'=4] {'row'}, use_global_device_ids=true, to_apply=%region_3.4 | all-reduce | flops 256 | bytes 2048 | tf_op jit(solution)/shard_map/psum | solution.py:36
  108.8 0.1 copy.11
  108.9 1.5 cholesky.16
  110.4 0.6 compare_reduce_fusion
  111.0 0.6 fusion.3
  111.7 1.2 custom-call.7
  112.9 0.3 fusion.4
  113.2 0.0 copy-start.1
  113.2 19.6 %convolution_bitcast_fusion = f32[4,2,8,2048]{3,2,1,0:T(8,128)S(1)} fusion(f32[4,1024,2048]{2,1,0:T(8,128)} %get-tuple-element.30, f32[16,1024]{1,0:T(8,128)S(1)} %fusion.4), kind=kOutput, calls=%fused_computation.2 | convolution fusion | flops 1610612736 | bytes 34144256 | tf_op jit(solution)/shard_map/km,bmw->kbw/dot_general | solution.py:39
  132.8 0.0 copy-done.1
  132.8 0.8 copy.15
  133.6 0.0 all-reduce.2.cloned.1.call-update
  133.6 55.5 %all-reduce.2.cloned.1.call-done = f32[16,8192]{1,0:T(8,128)} async-done(((f32[16,8192]{1,0:T(8,128)}), f32[16,8192]{1,0:T(8,128)}) %all-reduce.2.cloned.1.call-update) | async-done | bytes 524304 | tf_op jit(solution)/shard_map/psum | solution.py:42
  189.1 1.9 fusion.9
  191.1 11.8 %psum.23 = f32[16,16]{1,0:T(8,128)S(1)} all-reduce(f32[16,16]{1,0:T(8,128)S(1)} %fusion.9), channel_id=1, replica_groups=mesh['row'=8,'col'=4] {'col'}, use_global_device_ids=true, to_apply=%region_7.8 | all-reduce | flops 256 | bytes 2048 | tf_op jit(solution)/shard_map/psum | solution.py:43
  202.8 0.6 broadcast_multiply_fusion
  203.4 1.9 copy.28
  (6 shorter events, 0.1 us)
Async XLA Ops:
  7.2 182.0 %all-reduce.2.cloned.1.call-start = ((), (), s32[]{:S(2)}) async-start(), calls=%async_computation | async-start | bytes 1048576 | tf_op jit(solution)/shard_map/psum | solution.py:42
  7.2 43.4 %copy-start = (f32[16,8192]{1,0:T(8,128)S(1)}, f32[16,8192]{1,0:T(8,128)}, u32[]{:S(2)}) copy-start(f32[16,8192]{1,0:T(8,128)} %param.7) | copy-start | bytes 1572868
  113.2 19.6 %copy-start.1 = (f32[16,1024]{1,0:T(8,128)}, f32[16,1024]{1,0:T(8,128)S(1)}, u32[]{:S(2)}) copy-start(f32[16,1024]{1,0:T(8,128)S(1)} %fusion.4) | copy-start | bytes 196612
Sparse Core Ops, SparseCore 0:
  133.8 55.3 all-reduce.1
